TPU v7x, 1024 devices: a whole 4x4x32 slice. The times are simulated.
1024 devices in a mesh: section: 16 (over z_hi, y, core), dp: 64 (over z_lo, x).
Axes of the slice: x: 4, y: 4, z: 32 (z_hi: 2, z_lo: 16; z = z_hi * 16 + z_lo), core: 2. Of those that a mesh axis runs over, the one named last changes fastest.
Arguments:
- tokens: bfloat16 [512, 6144], P('dp', 'section'), may hold values from -6 to 6
- expert_ids: int32 [512, 2], P('dp'), may hold values from 0 to 7, all different within a row; in each aligned block of 8 rows (0 to 7, 8 to 15, ...) at most 4 rows name the same one
- router: bfloat16 [6144, 8], replicated, may hold values from -0.078125 to 0.078125
- w_up: bfloat16 [64, 6144, 2048], P('dp', None, 'section'), may hold values from -0.078125 to 0.078125
- w_down: bfloat16 [64, 2048, 6144], P('dp', 'section'), may hold values from -0.0625 to 0.0625
- attn_queries: bfloat16 [64, 128, 6144], P('dp', None, 'section'), may hold values from -140 to 140
- attn_keys: bfloat16 [64, 128, 6144], P('dp', None, 'section'), may hold values from -8 to 8
- attn_values: bfloat16 [64, 128, 6144], P('dp', None, 'section'), may hold values from -6 to 6
Outputs:
- mixed: bfloat16 [512, 6144], P('dp', 'section')
- attended: bfloat16 [64, 128, 6144], P('dp', None, 'section')
Inputs may be any that keep to these rules, and one draw needn't show every extreme that they name: `expert_ids`: each row names two different experts; among the 8 rows of one dp index (aligned blocks) no expert is named more than 4 times.
All inputs are finite; a program needn't handle non-finite values.
Results may differ from a plain program's by a relative error of at most 0.005.
Values may be sent and summed in bfloat16 or wider, within the bound.
A program may use at most 32 MiB of HBM per device.

v0:
```python
import math

import jax
import jax.numpy as jnp
from jax import lax
from jax.sharding import PartitionSpec as P

HEAD_DIM = 128
CAP = 4


def sent_to_all(x, axis):
    peers = lax.axis_size(axis)
    return lax.all_to_all(jnp.broadcast_to(x[None], (peers, *x.shape)), axis, 0, 0, tiled=True)


def taken_together(x, axis):
    return sent_to_all(x, axis).sum(axis=0)


def route_slots(expert_ids, block_count, per_block, experts):
    pair_ids = expert_ids.reshape(block_count, per_block * 2)
    onehot = (pair_ids[:, :, None] == jnp.arange(experts, dtype=jnp.int32)[None, None, :]).astype(
        jnp.int32
    )
    before = jnp.cumsum(onehot, axis=1) - onehot
    slot_rank = jnp.sum(before * onehot, axis=2)
    return slot_rank.reshape(block_count * per_block, 2)


def attend_head(operands):
    head_queries, head_keys, head_values = operands
    length = head_queries.shape[0]
    scores = jnp.dot(head_queries, head_keys.T, preferred_element_type=jnp.float32) * (
        1.0 / math.sqrt(head_queries.shape[1])
    )
    positions = jnp.arange(length, dtype=jnp.int32)
    causal = positions[None, :] <= positions[:, None]
    scores = jnp.where(causal, scores, -jnp.inf)
    row_max = jnp.max(scores, axis=1, keepdims=True)
    exp_scores = jnp.exp(scores - row_max)
    row_total = jnp.sum(exp_scores, axis=1, keepdims=True)
    probs = (exp_scores / row_total).astype(jnp.bfloat16)
    return jnp.dot(probs, head_values, preferred_element_type=jnp.float32).astype(jnp.bfloat16)


def local_attention(attn_queries, attn_keys, attn_values):
    batch, length, width = attn_queries.shape
    heads = width // HEAD_DIM

    def split_heads(array):
        return jnp.transpose(array.reshape(batch, length, heads, HEAD_DIM), (0, 2, 1, 3)).reshape(
            batch * heads, length, HEAD_DIM
        )

    outputs = lax.map(
        attend_head, (split_heads(attn_queries), split_heads(attn_keys), split_heads(attn_values))
    )
    return jnp.transpose(outputs.reshape(batch, heads, length, HEAD_DIM), (0, 2, 1, 3)).reshape(
        batch, length, width
    )


def per_device(tokens, expert_ids, router, w_up, w_down, attn_queries, attn_keys, attn_values):
    per_block, local_width = tokens.shape
    experts = router.shape[1]
    block_count = lax.axis_size("dp")
    split_count = block_count // experts
    cap_range = jnp.arange(CAP, dtype=jnp.int32)
    expert_range = jnp.arange(experts, dtype=jnp.int32)
    feature_start = lax.axis_index("section") * local_width
    router_rows = lax.dynamic_slice_in_dim(router, feature_start, local_width, 0)
    partial_logits = jnp.dot(tokens, router_rows, preferred_element_type=jnp.float32)
    logits = taken_together(partial_logits, "section")
    id_onehot = (expert_ids[:, :, None] == expert_range[None, None, :]).astype(jnp.float32)
    chosen = jnp.sum(logits[:, None, :] * id_onehot, axis=2)
    first_prob = jax.nn.sigmoid(chosen[:, 0] - chosen[:, 1])
    pair_prob = jnp.stack([first_prob, 1.0 - first_prob], axis=1)
    slot_rank = route_slots(expert_ids, 1, per_block, experts)
    matched = (expert_ids[:, :, None] == expert_range)[..., None] & (
        slot_rank[:, :, None, None] == cap_range
    )
    selector = jnp.any(matched, axis=1).astype(jnp.bfloat16)
    packed = jnp.einsum("tec,td->ecd", selector, tokens, preferred_element_type=jnp.float32).astype(
        jnp.bfloat16
    )
    outgoing = jnp.repeat(packed, split_count, axis=0)
    received = lax.all_to_all(outgoing, "dp", split_axis=0, concat_axis=0, tiled=True)
    flat_rows = received.reshape(block_count * CAP, local_width)
    up_weight = w_up[0]
    projected = jnp.dot(
        lax.all_gather(flat_rows, "section", axis=1, tiled=True),
        up_weight,
        preferred_element_type=jnp.float32,
    )
    activated = jax.nn.silu(projected).astype(jnp.bfloat16)
    model_width = w_down.shape[2]
    partial_value = jnp.dot(activated, w_down[0], preferred_element_type=jnp.float32).reshape(
        block_count, CAP, model_width
    )
    summed = lax.psum_scatter(partial_value, "section", scatter_dimension=2, tiled=True)
    returned = lax.all_to_all(summed, "dp", split_axis=0, concat_axis=0, tiled=True)
    attended = local_attention(attn_queries, attn_keys, attn_values)
    group_expert = jnp.arange(block_count, dtype=jnp.int32) // split_count
    on_expert = (expert_ids[:, :, None] == group_expert[None, None, :]).astype(jnp.float32)
    on_slot = (slot_rank[:, :, None] == cap_range[None, None, :]).astype(jnp.float32)
    coefficient = jnp.einsum(
        "tk,tkg,tkc->tgc", pair_prob, on_expert, on_slot, precision=lax.Precision.HIGHEST
    )
    mixed = jnp.einsum("tgc,gcd->td", coefficient, returned, precision=lax.Precision.HIGHEST)
    return (mixed.astype(jnp.bfloat16), attended)


def solution(mesh):
    placed = (
        P("dp", "section"),
        P("dp", None),
        P(),
        P("dp", None, "section"),
        P("dp", "section", None),
        P("dp", None, "section"),
        P("dp", None, "section"),
        P("dp", None, "section"),
    )
    return jax.shard_map(
        per_device,
        mesh=mesh,
        in_specs=placed,
        out_specs=(P("dp", "section"), P("dp", None, "section")),
        check_vma=False,
    )
```

profile of v0, /device:TPU:1, one launch (start us, length us, event | category | flops | bytes accessed | tf_op | source)
XLA Modules:
  0.0 596.1 jit_solution(17632698237035772756)
XLA Ops:
  7.2 0.0 copy-start
  7.2 0.0 all-gather.2.cloned.1.call-start
  7.2 0.9 copy.48
  8.1 0.8 iota_compare_fusion.1
  8.8 0.1 eq.94
  8.9 0.1 fusion.26
  9.0 0.2 select_reduce_fusion.1
  9.2 0.1 eq.98
  9.3 0.1 iota_compare_fusion.2
  9.4 0.1 copy.53
  9.5 0.1 and_reduce_fusion
  9.6 0.9 convolution_convert_fusion.1
  10.5 0.1 broadcast_in_dim.13
  10.6 55.5 %all_to_all.15 = bf16[64,4,384]{2,1,0:T(4,128)(2,1)S(1)} all-to-all(bf16[64,4,384]{2,1,0:T(4,128)(2,1)S(1)} %bitcast.54), channel_id=1, replica_groups=mesh['section'=16,'dp'=64] {'dp'}, dimensions={0} | all-to-all | bytes 393216 | tf_op jit(solution)/shard_map/all_to_all | solution.py:88
  66.0 0.7 reshape.147
  66.8 0.0 all-gather.2.cloned.1.call-update
  66.8 0.0 reduce-scatter.2.cloned.1.call-start
  66.8 169.5 %all-gather.2.cloned.1.call-done = bf16[256,6144]{1,0:T(8,128)(2,1)} async-done(((bf16[256,384]{1,0:T(8,128)(2,1)}), bf16[256,6144]{1,0:T(8,128)(2,1)}) %all-gather.2.cloned.1.call-update) | async-done | bytes 3145744 | tf_op jit(solution)/shard_map/all_gather | solution.py:92
  236.3 3.3 multiply_convert_fusion
  239.7 3.6 fusion.13
  243.3 0.0 reduce-scatter.2.cloned.1.call-update
  243.4 0.0 copy-start.2
  243.4 0.0 copy-start.3
  243.4 0.6 copy-done.4
  244.0 0.8 convolution_bitcast_fusion.1
  244.8 0.1 copy.50
  244.9 0.6 broadcast_in_dim.12
  245.5 4.2 all-to-all-start
  249.8 293.1 %reduce-scatter.2.cloned.1.call-done = f32[64,4,384]{2,0,1:T(8,128)} async-done(((f32[64,4,6144]{2,0,1:T(8,128)}), f32[64,4,384]{2,0,1:T(8,128)}) %reduce-scatter.2.cloned.1.call-update) | async-done | bytes 393232 | tf_op jit(solution)/shard_map/reduce_scatter | solution.py:101
  542.9 2.0 copy.57
  544.9 5.3 all-to-all-start.2
  550.3 0.0 copy-start.5
  550.3 1.7 while.10
  550.3 0.2 fusion.47
  550.6 0.2 fusion.49
  550.8 0.1 copy.73
  550.9 0.2 fusion.47
  551.2 0.2 fusion.49
  551.4 0.1 copy.73
  551.5 0.2 fusion.47
  551.7 0.2 fusion.49
  551.9 0.1 copy.73
  552.1 0.8 copy.61
  552.9 0.2 select_reduce_fusion
  553.1 0.1 copy.52
  553.1 0.3 fusion.23
  553.5 34.8 %all-to-all-done.2 = f32[64,4,384]{2,1,0:T(4,128)S(1)} async-done(((f32[64,4,384]{2,1,0:T(4,128)}), f32[64,4,384]{2,1,0:T(4,128)S(1)}, u32[]{:S(2)}, u32[]{:S(2)}) %all-to-all-start.2) | async-done | bytes 393248 | tf_op jit(solution)/shard_map/all_to_all | solution.py:102
  588.3 0.9 fusion.17
  (27 shorter events, 0.4 us)
Async XLA Ops:
  7.2 232.5 %copy-start = (bf16[1,128,6144]{2,1,0:T(8,128)(2,1)S(1)}, bf16[1,128,6144]{2,1,0:T(8,128)(2,1)}, u32[]{:S(2)}) copy-start(bf16[1,128,6144]{2,1,0:T(8,128)(2,1)} %param.14) | copy-start | bytes 4718596
  7.2 229.2 %all-gather.2.cloned.1.call-start = ((), (), s32[]{:S(2)}) async-start(), calls=%async_computation.4 | async-start | bytes 3342336 | tf_op jit(solution)/shard_map/all_gather | solution.py:92
  66.8 476.1 %reduce-scatter.2.cloned.1.call-start = ((), (), s32[]{:S(2)}) async-start(), calls=%async_computation.5 | async-start | bytes 6684672 | tf_op jit(solution)/shard_map/reduce_scatter | solution.py:101
  243.3 0.7 copy-start.4
  243.4 306.8 %copy-start.1 = (bf16[1,128,384]{2,1,0:T(8,128)(2,1)S(1)}, bf16[1,128,384]{2,1,0:T(8,128)(2,1)}, u32[]{:S(2)}) copy-start(bf16[1,128,384]{2,1,0:T(8,128)(2,1)} %param.15) | copy-start | bytes 294916
  243.4 306.9 %copy-start.2 = (bf16[1,128,384]{2,1,0:T(8,128)(2,1)S(1)}, bf16[1,128,384]{2,1,0:T(8,128)(2,1)}, u32[]{:S(2)}) copy-start(bf16[1,128,384]{2,1,0:T(8,128)(2,1)} %param.16) | copy-start | bytes 294916
  243.4 306.9 %copy-start.3 = (bf16[1,128,384]{2,1,0:T(8,128)(2,1)S(1)}, bf16[1,128,384]{2,1,0:T(8,128)(2,1)}, u32[]{:S(2)}) copy-start(bf16[1,128,384]{2,1,0:T(8,128)(2,1)} %param.17) | copy-start | bytes 294916
  245.5 299.3 %all-to-all-start = ((f32[16,8,8]{2,1,0:T(8,128)}), f32[16,8,8]{2,1,0:T(8,128)S(1)}, u32[]{:S(2)}, u32[]{:S(2)}) async-start(f32[16,8,8]{2,1,0:T(8,128)} %broadcast_in_dim.12), calls=%async_computation | async-start | bytes 131072 | tf_op jit(solution)/shard_map/all_to_all | solution.py:14
  544.9 43.5 %all-to-all-start.2 = ((f32[64,4,384]{2,1,0:T(4,128)}), f32[64,4,384]{2,1,0:T(4,128)S(1)}, u32[]{:S(2)}, u32[]{:S(2)}) async-start(f32[64,4,384]{2,1,0:T(4,128)} %copy.57), calls=%async_computation.3 | async-start | bytes 786432 | tf_op jit(solution)/shard_map/all_to_all | solution.py:102
  550.3 2.5 copy-start.5
Sparse Core Ops, SparseCore 0:
  66.9 169.3 all-gather.1
  243.5 299.3 reduce-scatter.1
where the time goes:
time: 603 us; the launch traced here: 596 us
  waiting for transfers between devices  497 us (82%)
  blocking collectives  55.5 us (9%)
  between operations  14.2 us (2%)
  matrix products  11.1 us (2%)
  starting transfers between devices  9.61 us (2%)
  local copies, waits for them, and re-layouts  6.55 us (1%)
    reduce_scatter x1, waiting for transfers between devices, per_device(): lax.psum_scatter(partial_value, 'section', scatter_dimension=2, tiled=True)  293 us
    all_gather x1, waiting for transfers between devices, per_device(): lax.all_gather(flat_rows, 'section', axis=1, tiled=True)  170 us
    all_to_all x1, blocking collectives, per_device(): lax.all_to_all(outgoing, 'dp', split_axis=0, concat_axis=0, tiled=True)  55.5 us
    all_to_all x1, waiting for transfers between devices, per_device(): lax.all_to_all(summed, 'dp', split_axis=0, concat_axis=0, tiled=True)  34.8 us
  transfers between devices with their start and end apart: 4, of which 3 were waited for; matrix products, arithmetic and copies ran while one was open for 1% of the time, Pallas kernels for 0%

commit v1 on v0

v1 whole, which is shorter than its diff:
```python
import functools
import math

import jax
import jax.numpy as jnp
from jax import lax
from jax.experimental import pallas as pl
from jax.experimental.pallas import tpu as pltpu
from jax.sharding import PartitionSpec as P

HEAD_DIM = 128
CAP = 4
WIDTH = 384
HIDDEN = 128
MESH = pl.DeviceIdType.MESH
F32, BF16 = jnp.float32, jnp.bfloat16

ORDER = (0, 1, 3, 2)
FAR_FIRST = (8, 7, 9, 6, 10, 5, 11, 4, 12, 3, 13, 2, 14, 1, 15)


def kernel(
    tok_ref, ids_ref, router_ref, up_ref, down_ref, q_hbm, k_hbm, v_hbm,
    mixed_ref, att_ref,
    q_ref, k_ref, v_ref, router_vm, w_up, w_down,
    rows32, pieces, z_in, x_all, h_own, h_in, act, o_all,
    r1, s1, r2, s2, r3, half16, z_out, z_back, gathered,
    logit_own, logit_far, logit_half, logit_in, logit_sum, logit_pair,
    load_sem, wu_sem, wd_sem,
    zs_sem, zr_sem,
    zp_s, zp_r, i_s, i_r, j_s, j_r, h_s, h_r,
    a_s, a_r, b_s, b_r, p_s, p_r, f_s, f_r,
    l_s, l_r,
):
    sec, dp = lax.axis_index("section"), lax.axis_index("dp")
    c = sec % 2
    y = (sec // 2) % 4
    h = sec // 8
    x = dp % 4
    zl = dp // 4
    p = zl % 2
    e = zl // 2
    z = h * 16 + zl
    b0 = z // 8
    i = x * (1 - c) + y * c
    j = y * (1 - c) + x * c

    def dev(x_, y_, z_, c_):
        return {"section": ((z_ // 16) * 4 + y_) * 2 + c_, "dp": (z_ % 16) * 4 + x_}

    def i_peer(d):
        return dev((x + d * (1 - c)) % 4, (y + d * c) % 4, z, c)

    def j_peer(d):
        return dev((x + d * c) % 4, (y + d * (1 - c)) % 4, z, c)

    partner = dev(x, y, z, 1 - c)
    z_pair = dev(x, y, z + 1 - 2 * p, c)
    z_opp = (z + 16) % 32

    def remote(src, dst, s, r, to):
        return pltpu.make_async_remote_copy(
            src_ref=src, dst_ref=dst, send_sem=s, recv_sem=r, device_id=to, device_id_type=MESH
        )

    def drain(ref, sem):
        pltpu.make_async_copy(ref, ref, sem).wait()

    barrier = pltpu.get_barrier_semaphore()
    peers = [dev(x, y, (z + 2 * m) % 32, c) for m in FAR_FIRST]
    peers += [i_peer(d) for d in (1, 2, 3)] + [j_peer(d) for d in (1, 2, 3)] + [z_pair, partner]
    for peer in peers:
        pl.semaphore_signal(barrier, inc=1, device_id=peer, device_id_type=MESH)

    loads = [
        pltpu.make_async_copy(router_ref.at[:, pl.ds(pl.multiple_of(sec * WIDTH, 128), WIDTH)], router_vm, load_sem.at[0]),
        pltpu.make_async_copy(q_hbm, q_ref, load_sem.at[1]),
        pltpu.make_async_copy(k_hbm, k_ref, load_sem.at[2]),
        pltpu.make_async_copy(v_hbm, v_ref, load_sem.at[3]),
    ]
    my_half = pl.ds(pl.multiple_of(c * HIDDEN, HIDDEN), HIDDEN)
    load_up = pltpu.make_async_copy(up_ref.at[:, c], w_up.at[:, :, my_half], wu_sem.at[0])
    for load in loads:
        load.start()
    load_up.start()

    def down_cols(block, core):
        start = pl.multiple_of((block * 2 + core) * WIDTH, 128)
        return down_ref.at[:, pl.ds(start, WIDTH)]

    for block in range(8):
        pltpu.make_async_copy(down_cols(block, c), w_down.at[block, my_half], wd_sem.at[0]).start()

    lane = lax.broadcasted_iota(jnp.int32, (32, 8), 1)
    row = lax.broadcasted_iota(jnp.int32, (32, 8), 0)
    row_expert = row // CAP
    first = (jnp.broadcast_to(ids_ref[0:1, :], (32, 8)) == row_expert).astype(F32)
    second = (jnp.broadcast_to(ids_ref[1:2, :], (32, 8)) == row_expert).astype(F32)
    hit = first + second
    rank = jnp.zeros((32, 8), F32)
    for t in range(7):
        before = jnp.broadcast_to(hit[:, t : t + 1], (32, 8))
        rank = rank + jnp.where(lane > t, before, 0.0)
    in_slot = jnp.where(rank == (row % CAP).astype(F32), hit, 0.0)
    rows32[...] = jnp.dot(in_slot, tok_ref[...].astype(F32), preferred_element_type=F32)
    for ex in range(8):
        pieces[ex] = rows32[pl.ds(CAP * ex, CAP), :].astype(BF16)
    loads[0].wait()
    logit_own[...] = lax.dot_general(
        router_vm[...], tok_ref[...], (((1,), (1,)), ((), ())), preferred_element_type=F32
    )

    pl.semaphore_wait(barrier, len(peers))

    my_slot = (z // 8) * 4 + (zl % 8) // 2
    for m in FAR_FIRST:
        zt = (z + 2 * m) % 32
        remote(
            pieces.at[(zt % 16) // 2], z_in.at[my_slot], zs_sem, zr_sem.at[b0], dev(x, y, zt, c)
        ).start()
    pltpu.make_async_copy(pieces.at[e], z_in.at[my_slot], zr_sem.at[b0]).start()
    remote(logit_own, logit_far, l_s.at[0], l_r.at[0], dev(x, y, z_opp, c)).start()

    send_up = remote(up_ref.at[:, 1 - c], w_up.at[:, :, my_half], wu_sem.at[1], wu_sem.at[2], partner)
    send_up.start()
    for block in range(8):
        remote(
            down_cols(block, 1 - c), w_down.at[block, my_half], wd_sem.at[1], wd_sem.at[2], partner
        ).start()

    for load in loads[1:]:
        load.wait()
    causal = lax.broadcasted_iota(jnp.int32, (128, 128), 1) <= lax.broadcasted_iota(jnp.int32, (128, 128), 0)
    for head in range(3):
        cols = slice(head * HEAD_DIM, (head + 1) * HEAD_DIM)
        scores = lax.dot_general(
            q_ref[:, cols], k_ref[:, cols], (((1,), (1,)), ((), ())), preferred_element_type=F32
        ) * (1.0 / math.sqrt(HEAD_DIM))
        scores = jnp.where(causal, scores, -jnp.inf)
        exp_scores = jnp.exp(scores - jnp.max(scores, axis=1, keepdims=True))
        probs = (exp_scores / jnp.sum(exp_scores, axis=1, keepdims=True)).astype(BF16)
        att_ref[:, cols] = jnp.dot(probs, v_ref[:, cols], preferred_element_type=F32).astype(BF16)

    blocks = [(b0 + o) % 4 for o in ORDER]
    mine16 = pl.ds(pl.multiple_of(p * 16, 16), 16)
    other16 = pl.ds(pl.multiple_of((1 - p) * 16, 16), 16)

    def from_z(k):
        b = blocks[k]
        drain(z_in.at[pl.ds(b * 4, 4)], zr_sem.at[b])
        for s in range(4):
            half16[pl.ds(CAP * s, CAP), :] = z_in[b * 4 + s].astype(F32)
        x_all[k, i, j, mine16, :] = half16[...].astype(BF16)
        strip = x_all.at[k, i, j, mine16]
        remote(strip, strip, zp_s.at[k], zp_r.at[k], z_pair).start()

    def from_pair(k):
        drain(x_all.at[k, i, j, other16], zp_r.at[k])
        tile = x_all.at[k, i, j]
        for d in (1, 2, 3):
            remote(tile, tile, i_s.at[k], i_r.at[k], i_peer(d)).start()

    def from_i(k):
        drain(x_all.at[k, 0, pl.ds(0, 3)], i_r.at[k])
        strip = x_all.at[k, :, j]
        for d in (1, 2, 3):
            remote(strip, strip, j_s.at[k], j_r.at[k], j_peer(d)).start()

    def up(k):
        drain(x_all.at[k, pl.ds(0, 3)], j_r.at[k])
        half = blocks[k] // 2
        total = None
        for ys in range(4):
            left = jnp.concatenate(
                [x_all[k, xs * (1 - c) + ys * c, ys * (1 - c) + xs * c] for xs in range(4)], axis=0
            )
            term = jnp.dot(left, w_up[half * 4 + ys], preferred_element_type=F32)
            total = term if total is None else total + term
        return total

    def swap_hidden(g, total):
        h_own[g] = total
        remote(h_own.at[g], h_in.at[g], h_s.at[g], h_r.at[g], partner).start()

    def activate(g):
        drain(h_in.at[g], h_r.at[g])
        v = h_own[g] + h_in[g]
        act[g] = (v / (1.0 + jnp.exp(-v))).astype(BF16)

    def down(k, g):
        half = blocks[k] // 2
        for yd in range(4):
            out = jnp.dot(act[g], w_down[half * 4 + yd], preferred_element_type=F32).astype(BF16)
            for xd in range(4):
                o_all[k, xd * (1 - c) + yd * c, yd * (1 - c) + xd * c] = out[xd * 32 : (xd + 1) * 32]
        for d in (2, 1, 3):
            remote(
                o_all.at[k, :, (j + d) % 4], r1.at[k, d - 1], a_s.at[k], a_r.at[k], j_peer(d)
            ).start()

    def sum_j(k):
        drain(r1.at[k], a_r.at[k])
        for n in range(4):
            s1[k, n] = (
                o_all[k, n, j].astype(F32)
                + r1[k, 0, n].astype(F32)
                + r1[k, 1, n].astype(F32)
                + r1[k, 2, n].astype(F32)
            ).astype(BF16)
        for d in (2, 1, 3):
            remote(s1.at[k, (i + d) % 4], r2.at[k, d - 1], b_s.at[k], b_r.at[k], i_peer(d)).start()

    def sum_i(k):
        drain(r2.at[k], b_r.at[k])
        s2[k] = (
            s1[k, i].astype(F32)
            + r2[k, 0].astype(F32)
            + r2[k, 1].astype(F32)
            + r2[k, 2].astype(F32)
        )
        remote(s2.at[k, other16], r3.at[k], p_s.at[k], p_r.at[k], z_pair).start()

    def sum_pair(k):
        drain(r3.at[k], p_r.at[k])
        half16[...] = s2[k, mine16, :] + r3[k]
        for s in range(4):
            z_out[k, s] = half16[pl.ds(CAP * s, CAP), :].astype(BF16)
        b = blocks[k]
        for s in range(4):
            zt = b * 8 + 2 * s + p
            target = z_back.at[h * 8 + e]

            @pl.when(zt != z)
            def _():
                remote(z_out.at[k, s], target, f_s, f_r, dev(x, y, zt, c)).start()

            @pl.when(zt == z)
            def _():
                pltpu.make_async_copy(z_out.at[k, s], target, f_r).start()

    from_z(0)
    from_pair(0)
    from_z(1)
    from_z(2)
    from_i(0)
    from_pair(1)
    from_pair(2)
    from_z(3)
    from_i(1)
    from_i(2)
    from_pair(3)

    drain(logit_far, l_r.at[0])
    logit_half[...] = logit_own[...] + logit_far[...]
    for d in (1, 2, 3):
        remote(
            logit_half, logit_in.at[d - 1], l_s.at[1], l_r.at[1], dev(x, (y + d) % 4, z, c)
        ).start()

    load_up.wait()
    send_up.wait_send()
    drain(w_up.at[:, :, pl.ds(0, HIDDEN)], wu_sem.at[2])
    near = up(0)
    from_i(3)
    beside = up(1)
    beside = beside + up(2)
    swap_hidden(1, beside)

    drain(w_down.at[:, pl.ds(0, HIDDEN)], wd_sem.at[0])
    drain(w_down.at[:, pl.ds(0, HIDDEN)], wd_sem.at[1])
    drain(w_down.at[:, pl.ds(0, HIDDEN)], wd_sem.at[2])
    activate(1)
    down(1, 1)
    down(2, 1)
    near = near + up(3)
    swap_hidden(0, near)
    sum_j(1)
    activate(0)
    down(3, 0)
    down(0, 0)
    sum_j(2)
    sum_i(1)
    sum_i(2)
    sum_j(3)
    sum_pair(1)
    sum_pair(2)
    sum_j(0)
    sum_i(3)
    sum_i(0)
    sum_pair(3)
    sum_pair(0)

    drain(logit_in, l_r.at[1])
    logit_sum[...] = logit_half[...] + logit_in[0] + logit_in[1] + logit_in[2]
    remote(logit_sum, logit_pair, l_s.at[2], l_r.at[2], partner).start()
    drain(logit_pair, l_r.at[2])
    full = logit_sum[...] + logit_pair[...]
    named = lax.broadcasted_iota(jnp.int32, (8, 8), 0)
    chosen0 = jnp.sum(jnp.where(named == ids_ref[0:1, :], full, 0.0), axis=0, keepdims=True)
    chosen1 = jnp.sum(jnp.where(named == ids_ref[1:2, :], full, 0.0), axis=0, keepdims=True)
    prob0 = jax.nn.sigmoid(chosen0 - chosen1)
    coefficient = in_slot * (first * prob0 + second * (1.0 - prob0))

    drain(z_back, f_r)
    for ex in range(8):
        gathered[pl.ds(CAP * ex, CAP), :] = z_back[ex].astype(F32) + z_back[8 + ex].astype(F32)
    mixed = lax.dot_general(
        coefficient, gathered[...], (((0,), (0,)), ((), ())), preferred_element_type=F32,
        precision=lax.Precision.HIGHEST,
    )
    mixed_ref[...] = mixed.astype(BF16)

    drain(z_in.at[pl.ds(0, 15)], zs_sem)
    drain(z_back.at[pl.ds(0, 15)], f_s)
    for k in range(4):
        drain(x_all.at[k, 0, 0, pl.ds(0, 16)], zp_s.at[k])
        drain(x_all.at[k, 0, pl.ds(0, 3)], i_s.at[k])
        drain(x_all.at[k, pl.ds(0, 3)], j_s.at[k])
        drain(r1.at[k], a_s.at[k])
        drain(r2.at[k], b_s.at[k])
        drain(r3.at[k], p_s.at[k])
    for g in range(2):
        drain(h_in.at[g], h_s.at[g])
    drain(logit_far, l_s.at[0])
    drain(logit_in, l_s.at[1])
    drain(logit_pair, l_s.at[2])


def per_device(tokens, expert_ids, router, w_up, w_down, attn_queries, attn_keys, attn_values):
    vmem = pl.BlockSpec(memory_space=pltpu.VMEM)
    hbm = pl.BlockSpec(memory_space=pl.ANY)
    dma, one = pltpu.SemaphoreType.DMA, pltpu.SemaphoreType.DMA
    mixed, attended = pl.pallas_call(
        kernel,
        name="window",
        out_shape=(
            jax.ShapeDtypeStruct((8, WIDTH), BF16),
            jax.ShapeDtypeStruct((128, WIDTH), BF16),
        ),
        in_specs=[vmem, vmem, hbm, hbm, hbm, hbm, hbm, hbm],
        out_specs=(vmem, vmem),
        scratch_shapes=[
            pltpu.VMEM((128, WIDTH), BF16),
            pltpu.VMEM((128, WIDTH), BF16),
            pltpu.VMEM((128, WIDTH), BF16),
            pltpu.VMEM((8, WIDTH), BF16),
            pltpu.VMEM((8, WIDTH, 256), BF16),
            pltpu.VMEM((8, 256, WIDTH), BF16),
            pltpu.VMEM((32, WIDTH), F32),
            pltpu.VMEM((8, CAP, WIDTH), BF16),
            pltpu.VMEM((16, CAP, WIDTH), BF16),
            pltpu.VMEM((4, 4, 4, 32, WIDTH), BF16),
            pltpu.VMEM((2, 128, 256), F32),
            pltpu.VMEM((2, 128, 256), F32),
            pltpu.VMEM((2, 128, 256), BF16),
            pltpu.VMEM((4, 4, 4, 32, WIDTH), BF16),
            pltpu.VMEM((4, 3, 4, 32, WIDTH), BF16),
            pltpu.VMEM((4, 4, 32, WIDTH), BF16),
            pltpu.VMEM((4, 3, 32, WIDTH), BF16),
            pltpu.VMEM((4, 32, WIDTH), F32),
            pltpu.VMEM((4, 16, WIDTH), F32),
            pltpu.VMEM((16, WIDTH), F32),
            pltpu.VMEM((4, 4, CAP, WIDTH), BF16),
            pltpu.VMEM((16, CAP, WIDTH), BF16),
            pltpu.VMEM((32, WIDTH), F32),
            pltpu.VMEM((8, 8), F32),
            pltpu.VMEM((8, 8), F32),
            pltpu.VMEM((8, 8), F32),
            pltpu.VMEM((3, 8, 8), F32),
            pltpu.VMEM((8, 8), F32),
            pltpu.VMEM((8, 8), F32),
            dma((4,)), dma((3,)), dma((3,)),
            one, dma((4,)),
            dma((4,)), dma((4,)), dma((4,)), dma((4,)), dma((4,)), dma((4,)), dma((2,)), dma((2,)),
            dma((4,)), dma((4,)), dma((4,)), dma((4,)), dma((4,)), dma((4,)), one, one,
            dma((3,)), dma((3,)),
        ],
        compiler_params=pltpu.CompilerParams(
            collective_id=0, has_side_effects=True, vmem_limit_bytes=67043328
        ),
    )(
        tokens,
        expert_ids.T,
        router.T,
        w_up.reshape(8, 2, WIDTH, HIDDEN),
        w_down.reshape(HIDDEN, 16 * WIDTH),
        attn_queries.reshape(128, WIDTH),
        attn_keys.reshape(128, WIDTH),
        attn_values.reshape(128, WIDTH),
    )
    return mixed, attended.reshape(1, 128, WIDTH)


def solution(mesh):
    placed = (
        P("dp", "section"),
        P("dp", None),
        P(),
        P("dp", None, "section"),
        P("dp", "section", None),
        P("dp", None, "section"),
        P("dp", None, "section"),
        P("dp", None, "section"),
    )
    return jax.shard_map(
        per_device,
        mesh=mesh,
        in_specs=placed,
        out_specs=(P("dp", "section"), P("dp", None, "section")),
        check_vma=False,
    )
```

time: 603 us -> 92.5 us (0.15); the launches traced: 596 us -> 91.8 us
  waiting for transfers between devices: 497 us -> 0 us
  Pallas kernels: 0 us -> 88.3 us
  blocking collectives: 55.5 us -> 0 us
  between operations: 14.2 us -> 0.64 us
  matrix products: 11.1 us -> 0 us
  starting transfers between devices: 9.61 us -> 0 us
    reduce_scatter x1 -> x0, waiting for transfers between devices: 293 us -> none  [per_device(): lax.psum_scatter(partial_value, 'section', scatter_dimension=2, tiled=True)]
    all_gather x1 -> x0, waiting for transfers between devices: 170 us -> none  [per_device(): lax.all_gather(flat_rows, 'section', axis=1, tiled=True)]
    pallas_call x0 -> x1, Pallas kernels: none -> 88.3 us  [per_device(): pl.pallas_call(kernel, name='window', out_shape=(jax.ShapeDtypeStruct((8,...]
    all_to_all x1 -> x0, blocking collectives: 55.5 us -> none  [per_device(): lax.all_to_all(outgoing, 'dp', split_axis=0, concat_axis=0, tiled=True)]
    all_to_all x2 -> x0, waiting for transfers between devices: 34.8 us -> none  [the longest x1 34.8 us: per_device(): lax.all_to_all(summed, 'dp', split_axis=0, concat_axis=0, tiled=True)]
    dot_general x12 -> x0, matrix products: 11.1 us -> none  [the longest x1 3.63 us: per_device(): jnp.dot(activated, w_down[0], preferred_element_type=jnp.float32)]
    all_to_all x2 -> x0, starting transfers between devices: 9.53 us -> none  [the longest x1 5.3 us: per_device(): lax.all_to_all(summed, 'dp', split_axis=0, concat_axis=0, tiled=True)]
  transfers between devices with their start and end apart: 4 -> 0, of which waited for: 3 -> 0; matrix products, arithmetic and copies ran while one was open for 1% -> 0% of each run, Pallas kernels for 0% -> 0%
where the time goes in v1:
time: 92.5 us; the launch traced here: 91.8 us
  Pallas kernels  88.3 us (95%)
  local copies, waits for them, and re-layouts  2.83 us (3%)
    pallas_call x1, Pallas kernels, per_device(): pl.pallas_call(kernel, name='window', out_shape=(jax.ShapeDtypeStruct((8,...  88.3 us
    unnamed x2, local copies, waits for them, and re-layouts  2.83 us

profile of v1, /device:TPU:1, one launch (start us, length us, event | category | flops | bytes accessed | tf_op | source)
XLA Modules:
  0.0 91.8 jit_solution(8372768730786095484)
XLA Ops:
  0.6 88.3 %window.1 = (bf16[8,384]{1,0:T(8,128)(2,1)}, bf16[128,384]{1,0:T(8,128)(2,1)}) custom-call(bf16[8,384]{1,0:T(8,128)(2,1)} %tok_ref.1, s32[2,8]{1,0:T(2,128)} %bitcast.15, bf16[8,6144]{1,0:T(8,128)(2,1)} %bitcast.10, bf16[8,2,384,128]{3,2,1,0:T(8,128)(2,1)} %bitcast.8, bf16[128,6144]{1,0:T(8,128)(2,1)} %bitcast.9, bf16[128,384]{1,0:T(8,128)(2,1)} %bitcast.11, ...), custom_call_target="tpu_custom_call" | custom-call | tf_op jit(solution)/shard_map/window/pallas_call | solution.py:333
  89.0 1.3 %copy.12 = bf16[8,384]{1,0:T(8,128)(2,1)} copy(bf16[8,384]{1,0:T(8,128)(2,1)} %get-tuple-element.8) | data formatting | bytes 12288
  90.3 1.5 %copy.13 = bf16[1,128,384]{2,1,0:T(8,128)(2,1)} copy(bf16[1,128,384]{2,1,0:T(8,128)(2,1)} %bitcast.14) | data formatting | bytes 196608

commit v2 on v1

--- a/solution.py
+++ b/solution.py
@@ -15,21 +15,20 @@
 MESH = pl.DeviceIdType.MESH
 F32, BF16 = jnp.float32, jnp.bfloat16
 
-ORDER = (0, 1, 3, 2)
-FAR_FIRST = (8, 7, 9, 6, 10, 5, 11, 4, 12, 3, 13, 2, 14, 1, 15)
+DIRECT = (4, -4, 3, -3, 2, -2, 1, -1)
 
 
 def kernel(
     tok_ref, ids_ref, router_ref, up_ref, down_ref, q_hbm, k_hbm, v_hbm,
     mixed_ref, att_ref,
     q_ref, k_ref, v_ref, router_vm, w_up, w_down,
-    rows32, pieces, z_in, x_all, h_own, h_in, act, o_all,
-    r1, s1, r2, s2, r3, half16, z_out, z_back, gathered,
+    rows32, pieces, z_relay, z_in, x_all, h_own, h_in, act, o_all,
+    r1, s1, r2, half16, z_out, z_back, gathered,
     logit_own, logit_far, logit_half, logit_in, logit_sum, logit_pair,
     load_sem, wu_sem, wd_sem,
-    zs_sem, zr_sem,
-    zp_s, zp_r, i_s, i_r, j_s, j_r, h_s, h_r,
-    a_s, a_r, b_s, b_r, p_s, p_r, f_s, f_r,
+    zs_sem, zr_sem, relay_sem, forward_sem,
+    i_s, i_r, j_s, j_r, h_s, h_r,
+    a_s, a_r, b_s, b_r, f_s, f_r,
     l_s, l_r,
 ):
     sec, dp = lax.axis_index("section"), lax.axis_index("dp")
@@ -48,14 +47,14 @@
     def dev(x_, y_, z_, c_):
         return {"section": ((z_ // 16) * 4 + y_) * 2 + c_, "dp": (z_ % 16) * 4 + x_}
 
-    def i_peer(d):
-        return dev((x + d * (1 - c)) % 4, (y + d * c) % 4, z, c)
+    def i_peer(d, flip):
+        plane = z + flip * (1 - 2 * p)
+        return dev((x + d * (1 - c)) % 4, (y + d * c) % 4, plane, c)
 
     def j_peer(d):
         return dev((x + d * c) % 4, (y + d * (1 - c)) % 4, z, c)
 
     partner = dev(x, y, z, 1 - c)
-    z_pair = dev(x, y, z + 1 - 2 * p, c)
     z_opp = (z + 16) % 32
 
     def remote(src, dst, s, r, to):
@@ -67,8 +66,9 @@
         pltpu.make_async_copy(ref, ref, sem).wait()
 
     barrier = pltpu.get_barrier_semaphore()
-    peers = [dev(x, y, (z + 2 * m) % 32, c) for m in FAR_FIRST]
-    peers += [i_peer(d) for d in (1, 2, 3)] + [j_peer(d) for d in (1, 2, 3)] + [z_pair, partner]
+    around = [(2, 0), (2, 1), (1, 1), (3, 1), (1, 0), (3, 0), (0, 1)]
+    peers = [dev(x, y, (z + 2 * m + 32) % 32, c) for m in DIRECT]
+    peers += [i_peer(d, flip) for d, flip in around] + [j_peer(d) for d in (1, 2, 3)] + [partner]
     for peer in peers:
         pl.semaphore_signal(barrier, inc=1, device_id=peer, device_id_type=MESH)
 
@@ -112,14 +112,21 @@
 
     pl.semaphore_wait(barrier, len(peers))
 
-    my_slot = (z // 8) * 4 + (zl % 8) // 2
-    for m in FAR_FIRST:
-        zt = (z + 2 * m) % 32
+    place = (z % 8) // 2
+
+    def piece_for(m):
+        return pieces.at[((z + 2 * m + 32) % 16) // 2]
+
+    up_z, down_z = dev(x, y, (z + 8) % 32, c), dev(x, y, (z + 24) % 32, c)
+    for n in (3, 2, 1, 0):
+        remote(piece_for(5 + n), z_relay.at[n], zs_sem, relay_sem.at[0], up_z).start()
+    for n in (2, 1, 0):
+        remote(piece_for(-5 - n), z_relay.at[4 + n], zs_sem, relay_sem.at[1], down_z).start()
+    for m in DIRECT:
         remote(
-            pieces.at[(zt % 16) // 2], z_in.at[my_slot], zs_sem, zr_sem.at[b0], dev(x, y, zt, c)
+            piece_for(m), z_in.at[b0 * 4 + place], zs_sem, zr_sem.at[b0], dev(x, y, (z + 2 * m + 32) % 32, c)
         ).start()
-    pltpu.make_async_copy(pieces.at[e], z_in.at[my_slot], zr_sem.at[b0]).start()
-    remote(logit_own, logit_far, l_s.at[0], l_r.at[0], dev(x, y, z_opp, c)).start()
+    pltpu.make_async_copy(pieces.at[e], z_in.at[b0 * 4 + place], zr_sem.at[b0]).start()
 
     send_up = remote(up_ref.at[:, 1 - c], w_up.at[:, :, my_half], wu_sem.at[1], wu_sem.at[2], partner)
     send_up.start()
@@ -141,34 +148,42 @@
         probs = (exp_scores / jnp.sum(exp_scores, axis=1, keepdims=True)).astype(BF16)
         att_ref[:, cols] = jnp.dot(probs, v_ref[:, cols], preferred_element_type=F32).astype(BF16)
 
-    blocks = [(b0 + o) % 4 for o in ORDER]
     mine16 = pl.ds(pl.multiple_of(p * 16, 16), 16)
-    other16 = pl.ds(pl.multiple_of((1 - p) * 16, 16), 16)
-
-    def from_z(k):
-        b = blocks[k]
+
+    def forward():
+        drain(z_relay.at[pl.ds(0, 4)], relay_sem.at[0])
+        source = (b0 + 3) % 4
+        for n in (3, 2, 1, 0):
+            remote(
+                z_relay.at[n], z_in.at[source * 4 + place], forward_sem, zr_sem.at[source],
+                dev(x, y, (z + 2 + 2 * n) % 32, c),
+            ).start()
+        drain(z_relay.at[pl.ds(0, 3)], relay_sem.at[1])
+        source = (b0 + 1) % 4
+        for n in (2, 1, 0):
+            remote(
+                z_relay.at[4 + n], z_in.at[source * 4 + place], forward_sem, zr_sem.at[source],
+                dev(x, y, (z + 30 - 2 * n) % 32, c),
+            ).start()
+
+    def from_z(b):
         drain(z_in.at[pl.ds(b * 4, 4)], zr_sem.at[b])
         for s in range(4):
             half16[pl.ds(CAP * s, CAP), :] = z_in[b * 4 + s].astype(F32)
-        x_all[k, i, j, mine16, :] = half16[...].astype(BF16)
-        strip = x_all.at[k, i, j, mine16]
-        remote(strip, strip, zp_s.at[k], zp_r.at[k], z_pair).start()
-
-    def from_pair(k):
-        drain(x_all.at[k, i, j, other16], zp_r.at[k])
-        tile = x_all.at[k, i, j]
-        for d in (1, 2, 3):
-            remote(tile, tile, i_s.at[k], i_r.at[k], i_peer(d)).start()
-
-    def from_i(k):
-        drain(x_all.at[k, 0, pl.ds(0, 3)], i_r.at[k])
-        strip = x_all.at[k, :, j]
-        for d in (1, 2, 3):
-            remote(strip, strip, j_s.at[k], j_r.at[k], j_peer(d)).start()
+        x_all[b, i, j, mine16, :] = half16[...].astype(BF16)
+        strip = x_all.at[b, i, j, mine16]
+        for d, flip in around:
+            remote(strip, strip, i_s.at[b], i_r.at[b], i_peer(d, flip)).start()
+
+    def from_i(b):
+        drain(r2.at[b], i_r.at[b])
+        strip = x_all.at[b, :, j]
+        for d in (2, 1, 3):
+            remote(strip, strip, j_s.at[b], j_r.at[b], j_peer(d)).start()
 
     def up(k):
         drain(x_all.at[k, pl.ds(0, 3)], j_r.at[k])
-        half = blocks[k] // 2
+        half = k // 2
         total = None
         for ys in range(4):
             left = jnp.concatenate(
@@ -188,7 +203,7 @@
         act[g] = (v / (1.0 + jnp.exp(-v))).astype(BF16)
 
     def down(k, g):
-        half = blocks[k] // 2
+        half = k // 2
         for yd in range(4):
             out = jnp.dot(act[g], w_down[half * 4 + yd], preferred_element_type=F32).astype(BF16)
             for xd in range(4):
@@ -207,27 +222,22 @@
                 + r1[k, 1, n].astype(F32)
                 + r1[k, 2, n].astype(F32)
             ).astype(BF16)
-        for d in (2, 1, 3):
-            remote(s1.at[k, (i + d) % 4], r2.at[k, d - 1], b_s.at[k], b_r.at[k], i_peer(d)).start()
+        for d, flip in around:
+            rows = pl.ds(pl.multiple_of(((p + flip) % 2) * 16, 16), 16)
+            remote(
+                s1.at[k, (i + d) % 4, rows], r2.at[k, d * 2 + flip - 1], b_s.at[k], b_r.at[k], i_peer(d, flip)
+            ).start()
 
     def sum_i(k):
         drain(r2.at[k], b_r.at[k])
-        s2[k] = (
-            s1[k, i].astype(F32)
-            + r2[k, 0].astype(F32)
-            + r2[k, 1].astype(F32)
-            + r2[k, 2].astype(F32)
-        )
-        remote(s2.at[k, other16], r3.at[k], p_s.at[k], p_r.at[k], z_pair).start()
-
-    def sum_pair(k):
-        drain(r3.at[k], p_r.at[k])
-        half16[...] = s2[k, mine16, :] + r3[k]
+        total = s1[k, i, mine16, :].astype(F32)
+        for n in range(7):
+            total = total + r2[k, n].astype(F32)
+        half16[...] = total
         for s in range(4):
             z_out[k, s] = half16[pl.ds(CAP * s, CAP), :].astype(BF16)
-        b = blocks[k]
         for s in range(4):
-            zt = b * 8 + 2 * s + p
+            zt = k * 8 + 2 * s + p
             target = z_back.at[h * 8 + e]
 
             @pl.when(zt != z)
@@ -238,17 +248,38 @@
             def _():
                 pltpu.make_async_copy(z_out.at[k, s], target, f_r).start()
 
-    from_z(0)
-    from_pair(0)
-    from_z(1)
-    from_z(2)
-    from_i(0)
-    from_pair(1)
-    from_pair(2)
-    from_z(3)
-    from_i(1)
-    from_i(2)
-    from_pair(3)
+    odd = b0 % 2
+    opposite = (b0 + 2) % 4
+    order = [b0, (1 - odd) * opposite, 1 + odd, (1 - odd) * 3 + odd * opposite]
+    forward()
+    from_z(order[0])
+    from_i(order[0])
+    from_z(order[1])
+    from_z(order[2])
+    from_i(order[1])
+    from_z(order[3])
+    from_i(order[2])
+    from_i(order[3])
+    remote(logit_own, logit_far, l_s.at[0], l_r.at[0], dev(x, y, z_opp, c)).start()
+
+    load_up.wait()
+    send_up.wait_send()
+    drain(w_up.at[:, :, pl.ds(0, HIDDEN)], wu_sem.at[2])
+    swap_hidden(0, up(0) + up(2))
+    drain(w_down.at[:, pl.ds(0, HIDDEN)], wd_sem.at[0])
+    drain(w_down.at[:, pl.ds(0, HIDDEN)], wd_sem.at[1])
+    drain(w_down.at[:, pl.ds(0, HIDDEN)], wd_sem.at[2])
+    activate(0)
+    down(0, 0)
+    swap_hidden(1, up(1) + up(3))
+    sum_j(0)
+    activate(1)
+    down(1, 1)
+    sum_i(0)
+    down(2, 0)
+    sum_j(1)
+    down(3, 1)
+    sum_i(1)
 
     drain(logit_far, l_r.at[0])
     logit_half[...] = logit_own[...] + logit_far[...]
@@ -256,43 +287,14 @@
         remote(
             logit_half, logit_in.at[d - 1], l_s.at[1], l_r.at[1], dev(x, (y + d) % 4, z, c)
         ).start()
-
-    load_up.wait()
-    send_up.wait_send()
-    drain(w_up.at[:, :, pl.ds(0, HIDDEN)], wu_sem.at[2])
-    near = up(0)
-    from_i(3)
-    beside = up(1)
-    beside = beside + up(2)
-    swap_hidden(1, beside)
-
-    drain(w_down.at[:, pl.ds(0, HIDDEN)], wd_sem.at[0])
-    drain(w_down.at[:, pl.ds(0, HIDDEN)], wd_sem.at[1])
-    drain(w_down.at[:, pl.ds(0, HIDDEN)], wd_sem.at[2])
-    activate(1)
-    down(1, 1)
-    down(2, 1)
-    near = near + up(3)
-    swap_hidden(0, near)
-    sum_j(1)
-    activate(0)
-    down(3, 0)
-    down(0, 0)
     sum_j(2)
-    sum_i(1)
-    sum_i(2)
     sum_j(3)
-    sum_pair(1)
-    sum_pair(2)
-    sum_j(0)
-    sum_i(3)
-    sum_i(0)
-    sum_pair(3)
-    sum_pair(0)
-
     drain(logit_in, l_r.at[1])
     logit_sum[...] = logit_half[...] + logit_in[0] + logit_in[1] + logit_in[2]
     remote(logit_sum, logit_pair, l_s.at[2], l_r.at[2], partner).start()
+    sum_i(2)
+    sum_i(3)
+
     drain(logit_pair, l_r.at[2])
     full = logit_sum[...] + logit_pair[...]
     named = lax.broadcasted_iota(jnp.int32, (8, 8), 0)
@@ -312,13 +314,12 @@
 
     drain(z_in.at[pl.ds(0, 15)], zs_sem)
     drain(z_back.at[pl.ds(0, 15)], f_s)
+    drain(z_relay, forward_sem)
     for k in range(4):
-        drain(x_all.at[k, 0, 0, pl.ds(0, 16)], zp_s.at[k])
-        drain(x_all.at[k, 0, pl.ds(0, 3)], i_s.at[k])
-        drain(x_all.at[k, pl.ds(0, 3)], j_s.at[k])
+        drain(r2.at[k], i_s.at[k])
+        drain(r1.at[k], j_s.at[k])
         drain(r1.at[k], a_s.at[k])
         drain(r2.at[k], b_s.at[k])
-        drain(r3.at[k], p_s.at[k])
     for g in range(2):
         drain(h_in.at[g], h_s.at[g])
     drain(logit_far, l_s.at[0])
@@ -348,6 +349,7 @@
             pltpu.VMEM((8, 256, WIDTH), BF16),
             pltpu.VMEM((32, WIDTH), F32),
             pltpu.VMEM((8, CAP, WIDTH), BF16),
+            pltpu.VMEM((7, CAP, WIDTH), BF16),
             pltpu.VMEM((16, CAP, WIDTH), BF16),
             pltpu.VMEM((4, 4, 4, 32, WIDTH), BF16),
             pltpu.VMEM((2, 128, 256), F32),
@@ -356,9 +358,7 @@
             pltpu.VMEM((4, 4, 4, 32, WIDTH), BF16),
             pltpu.VMEM((4, 3, 4, 32, WIDTH), BF16),
             pltpu.VMEM((4, 4, 32, WIDTH), BF16),
-            pltpu.VMEM((4, 3, 32, WIDTH), BF16),
-            pltpu.VMEM((4, 32, WIDTH), F32),
-            pltpu.VMEM((4, 16, WIDTH), F32),
+            pltpu.VMEM((4, 7, 16, WIDTH), BF16),
             pltpu.VMEM((16, WIDTH), F32),
             pltpu.VMEM((4, 4, CAP, WIDTH), BF16),
             pltpu.VMEM((16, CAP, WIDTH), BF16),
@@ -370,9 +370,9 @@
             pltpu.VMEM((8, 8), F32),
             pltpu.VMEM((8, 8), F32),
             dma((4,)), dma((3,)), dma((3,)),
-            one, dma((4,)),
-            dma((4,)), dma((4,)), dma((4,)), dma((4,)), dma((4,)), dma((4,)), dma((2,)), dma((2,)),
-            dma((4,)), dma((4,)), dma((4,)), dma((4,)), dma((4,)), dma((4,)), one, one,
+            one, dma((4,)), dma((2,)), one,
+            dma((4,)), dma((4,)), dma((4,)), dma((4,)), dma((2,)), dma((2,)),
+            dma((4,)), dma((4,)), dma((4,)), dma((4,)), one, one,
             dma((3,)), dma((3,)),
         ],
         compiler_params=pltpu.CompilerParams(

time: 92.5 us -> 78.3 us (0.85)
  the two profiles are of different devices: /device:TPU:1 before, /device:TPU:8 now
where the time goes in v2:
time: 78.3 us; the launch traced here: 78.1 us
  Pallas kernels  74.6 us (95%)
  local copies, waits for them, and re-layouts  2.83 us (4%)
    pallas_call x1, Pallas kernels, per_device(): pl.pallas_call(kernel, name='window', out_shape=(jax.ShapeDtypeStruct((8,...  74.6 us
    unnamed x2, local copies, waits for them, and re-layouts  2.83 us

profile of v2, /device:TPU:8, one launch (start us, length us, event | category | flops | bytes accessed | tf_op | source)
XLA Modules:
  0.0 78.1 jit_solution(7219259109431279199)
XLA Ops:
  0.6 74.6 %window.1 = (bf16[8,384]{1,0:T(8,128)(2,1)}, bf16[128,384]{1,0:T(8,128)(2,1)}) custom-call(bf16[8,384]{1,0:T(8,128)(2,1)} %tok_ref.1, s32[2,8]{1,0:T(2,128)} %bitcast.15, bf16[8,6144]{1,0:T(8,128)(2,1)} %bitcast.10, bf16[8,2,384,128]{3,2,1,0:T(8,128)(2,1)} %bitcast.8, bf16[128,6144]{1,0:T(8,128)(2,1)} %bitcast.9, bf16[128,384]{1,0:T(8,128)(2,1)} %bitcast.11, ...), custom_call_target="tpu_custom_call" | custom-call | tf_op jit(solution)/shard_map/window/pallas_call | solution.py:334
  75.2 1.3 %copy.12 = bf16[8,384]{1,0:T(8,128)(2,1)} copy(bf16[8,384]{1,0:T(8,128)(2,1)} %get-tuple-element.8) | data formatting | bytes 12288
  76.5 1.5 %copy.13 = bf16[1,128,384]{2,1,0:T(8,128)(2,1)} copy(bf16[1,128,384]{2,1,0:T(8,128)(2,1)} %bitcast.14) | data formatting | bytes 196608
